TPU v7x, 256 devices: a whole 4x4x8 slice. The times are simulated.
256 devices in a mesh: section: 2 (over x_hi), feat: 16 (over y, x_lo, core), width: 8 (over z).
Axes of the slice: x: 4 (x_hi: 2, x_lo: 2; x = x_hi * 2 + x_lo), y: 4, z: 8, core: 2. Of those that a mesh axis runs over, the one named last changes fastest.
Arguments:
- mlp_inputs: bfloat16 [4, 1024, 2304], P('section', 'width'), may hold values from -6 to 6
- encoder: bfloat16 [4, 2304, 16384], P('section', 'width', 'feat'), may hold values from -0.125 to 0.125
- enc_bias: float32 [4, 16384], P('section', 'feat'), may hold values from -3 to 3
- decoder: bfloat16 [10, 16384, 2304], P('section', 'feat', 'width'), may hold values from -0.046875 to 0.046875
- dec_bias: float32 [4, 2304], P(None, 'width'), may hold values from -3 to 3
- targets: bfloat16 [4, 1024, 2304], P(None, None, 'width'), may hold values from -6 to 6
- live_rows: int32 [1024], replicated, may hold values 0 or 1
Outputs:
- errors: bfloat16 [4, 1024, 2304], P(None, None, 'width')
- gradients: bfloat16 [10, 16384, 2304], P('section', 'feat', 'width')
All inputs are finite; a program needn't handle non-finite values.
Results may differ from a plain program's by a relative error of at most 0.0042.
Values may be sent and summed in bfloat16 or wider, within the bound.
No kernel may reach another device: no remote copies, remote signals or barrier semaphores. Data moves between devices by JAX's collectives and lax.ppermute only.
A program may use at most 128 MiB of HBM per device.

v0:
```python
import jax
import jax.numpy as jnp
from jax import lax
from jax.sharding import PartitionSpec as P


def from_behind(value, axis, steps):
    count = lax.axis_size(axis)
    initial, last = (max(0, -steps), min(count, count - steps))
    return lax.ppermute(value, axis, [(source, source + steps) for source in range(initial, last)])


def pair_tables(layer_count):
    source_ids = []
    target_ids = []
    for source in range(layer_count):
        for target in range(source, layer_count):
            source_ids.append(source)
            target_ids.append(target)
    return (jnp.array(source_ids, jnp.int32), jnp.array(target_ids, jnp.int32))


def local(mlp_inputs, encoder, enc_bias, decoder, dec_bias, targets, live_rows):
    layers_here, tok_local, model_width = mlp_inputs.shape
    pre_act = jnp.einsum(
        "ltd,ldf->tlf",
        mlp_inputs,
        lax.all_gather(encoder, "width", axis=1, tiled=True),
        preferred_element_type=jnp.float32,
    )
    local_feats = jnp.maximum(pre_act + enc_bias[None, :, :], 0.0).astype(jnp.bfloat16)
    token_feats = lax.all_gather(local_feats, "width", axis=0, tiled=True)
    layers_all = dec_bias.shape[0]
    tokens_all = live_rows.shape[0]
    per_section = decoder.shape[0]
    source_ids, target_ids = pair_tables(layers_all)
    section_id = lax.axis_index("section")
    earlier = from_behind(token_feats[:, layers_here - 1], "section", 1)
    features = jnp.concatenate([earlier[:, None, :], token_feats], axis=1)
    first_layer = section_id * layers_here - 1
    rebuilt = jnp.zeros((layers_all, tokens_all, decoder.shape[2]), jnp.float32)
    chosen = []
    for pair_slot in range(per_section):
        pair_id = section_id * per_section + pair_slot
        source = source_ids[pair_id]
        target = target_ids[pair_id]
        picked = lax.dynamic_index_in_dim(features, source - first_layer, 1, keepdims=False)
        chosen.append((picked, target))
        partial_value = jnp.dot(picked, decoder[pair_slot], preferred_element_type=jnp.float32)
        current = lax.dynamic_index_in_dim(rebuilt, target, 0, keepdims=False)
        rebuilt = lax.dynamic_update_index_in_dim(rebuilt, current + partial_value, target, 0)
    summed = lax.psum(rebuilt, ("section", "feat"))
    keep_rows = live_rows.astype(jnp.float32)[None, :, None]
    errors = ((summed + dec_bias[:, None, :] - targets.astype(jnp.float32)) * keep_rows).astype(
        jnp.bfloat16
    )
    gradients = []
    for picked, target in chosen:
        residual = lax.dynamic_index_in_dim(errors, target, 0, keepdims=False)
        product = lax.dot_general(
            picked, residual, (((0,), (0,)), ((), ())), preferred_element_type=jnp.float32
        )
        gradients.append((product / tokens_all).astype(jnp.bfloat16))
    return (errors, jnp.stack(gradients))


def solution(mesh):
    placed = (
        P("section", "width", None),
        P("section", "width", "feat"),
        P("section", "feat"),
        P("section", "feat", "width"),
        P(None, "width"),
        P(None, None, "width"),
        P(),
    )
    return jax.shard_map(
        local,
        mesh=mesh,
        in_specs=placed,
        out_specs=(P(None, None, "width"), P("section", "feat", "width")),
        check_vma=False,
    )
```

profile of v0, /device:TPU:1, one launch (start us, length us, event | category | flops | bytes accessed | tf_op | source)
XLA Modules:
  0.0 397.8 jit_solution(8431505922366384273)
XLA Ops:
  7.2 0.0 copy-start
  7.2 0.0 all-gather.3.cloned.1.call-start
  7.2 0.7 all-gather.3.cloned.1.call-update
  7.9 0.0 all-gather.5.cloned.1.call-start
  8.0 109.4 %all-gather.3.cloned.1.call-done = bf16[2,2304,1024]{2,1,0:T(8,128)(2,1)} async-done(((bf16[2,288,1024]{2,1,0:T(8,128)(2,1)}), bf16[2,2304,1024]{2,1,0:T(8,128)(2,1)}) %all-gather.3.cloned.1.call-update) | async-done | bytes 9437200 | tf_op jit(solution)/shard_map/all_gather | solution.py:28
  117.3 0.0 copy-done
  117.3 7.3 %fusion.36 = bf16[128,2,1024]{0,2,1:T(8,128)(2,1)} fusion(bf16[2,2304,1024]{2,1,0:T(8,128)(2,1)} %all-gather.3.cloned.1.call-done, bf16[2,128,2304]{2,1,0:T(8,128)(2,1)S(1)} %copy-done, f32[2,1024]{1,0:T(2,128)} %param.11), kind=kOutput, calls=%fused_computation.59 | convolution fusion | flops 1208745984 | bytes 11149312 | tf_op jit(solution)/shard_map/ltd,ldf->tlf/dot_general | solution.py:25
  124.7 0.0 copy-start.5
  124.7 0.0 copy-start.6
  124.7 0.0 all-gather.5.cloned.1.call-update
  124.7 0.0 all-reduce.2.cloned.1.call-start
  124.7 57.6 %all-gather.5.cloned.1.call-done = bf16[1024,2,1024]{0,2,1:T(8,128)(2,1)} async-done(((bf16[128,2,1024]{0,2,1:T(8,128)(2,1)}), bf16[1024,2,1024]{0,2,1:T(8,128)(2,1)}) %all-gather.5.cloned.1.call-update) | async-done | bytes 4194320 | tf_op jit(solution)/shard_map/all_gather | solution.py:32
  182.4 3.1 slice_bitcast_fusion
  185.4 4.4 %collective-permute-start = (bf16[1024,1024]{0,1:T(8,128)(2,1)}, bf16[1024,1024]{0,1:T(8,128)(2,1)S(1)}, u32[]{:S(2)}, u32[]{:S(2)}) collective-permute-start(bf16[1024,1024]{0,1:T(8,128)(2,1)} %slice_bitcast_fusion), channel_id=1, source_target_pairs={{0,128},{1,129},{2,130},{3,131},{4,132},{5,133},{6,134},{7,135},{8... | collective-permute-start | bytes 6291464 | tf_op jit(solution)/shard_map/ppermute | solution.py:10
  189.9 0.0 copy-done.5
  189.9 0.0 copy-done.6
  189.9 0.7 fusion.72
  203.2 26.7 %collective-permute-done = bf16[1024,1024]{0,1:T(8,128)(2,1)S(1)} collective-permute-done((bf16[1024,1024]{0,1:T(8,128)(2,1)}, bf16[1024,1024]{0,1:T(8,128)(2,1)S(1)}, u32[]{:S(2)}, u32[]{:S(2)}) %collective-permute-start) | collective-permute-done | bytes 2097184 | tf_op jit(solution)/shard_map/ppermute | solution.py:10
  229.9 0.0 copy-start.1
  229.9 3.0 broadcast_in_dim.25
  232.9 0.8 copy-done.1
  233.7 0.0 copy-start.3
  233.7 3.4 fusion.18
  237.1 1.3 constant_dynamic-slice_fusion.3
  238.5 0.0 copy-done.3
  238.5 2.2 fusion.17
  240.7 1.3 constant_dynamic-slice_fusion.2
  242.1 2.2 fusion.15
  244.3 1.3 constant_dynamic-slice_fusion.1
  245.6 2.3 fusion.13
  247.9 1.3 constant_dynamic-slice_fusion
  249.3 2.2 fusion.11
  251.5 0.0 copy-start.8
  251.5 0.0 copy-start.7
  251.5 0.0 all-reduce.2.cloned.1.call-update
  251.5 0.7 copy-done.8
  252.2 126.4 %all-reduce.2.cloned.1.call-done = f32[4,1024,288]{1,2,0:T(8,128)} async-done(((f32[4,1024,288]{1,2,0:T(8,128)}), f32[4,1024,288]{1,2,0:T(8,128)}) %all-reduce.2.cloned.1.call-update) | async-done | bytes 4718608 | tf_op jit(solution)/shard_map/psum | solution.py:52
  378.6 0.0 copy-done.7
  378.6 0.0 copy-start.2
  378.6 3.9 multiply_convert_fusion
  382.5 0.3 copy-done.2
  382.8 0.0 copy-start.4
  382.8 1.4 fusion.35
  384.2 1.4 fusion.33
  385.6 1.4 fusion.31
  386.9 1.4 fusion.29
  388.3 0.0 copy-done.4
  388.3 1.4 fusion.27
  389.7 0.0 copy-start.9
  389.7 1.6 copy-done.9
  (1 shorter events, 0.0 us)
Async XLA Ops:
  7.2 110.2 %copy-start = (bf16[2,128,2304]{2,1,0:T(8,128)(2,1)S(1)}, bf16[2,128,2304]{2,1,0:T(8,128)(2,1)}, u32[]{:S(2)}) copy-start(bf16[2,128,2304]{2,1,0:T(8,128)(2,1)} %param.9) | copy-start | bytes 3538948
  7.2 110.2 %all-gather.3.cloned.1.call-start = ((), (), s32[]{:S(2)}) async-start(), calls=%async_computation | async-start | bytes 10616832 | tf_op jit(solution)/shard_map/all_gather | solution.py:28
  7.9 174.4 %all-gather.5.cloned.1.call-start = ((), (), s32[]{:S(2)}) async-start(), calls=%async_computation.1 | async-start | bytes 4718592 | tf_op jit(solution)/shard_map/all_gather | solution.py:32
  124.7 65.2 %copy-start.5 = (s32[10]{0:T(128)S(1)}, s32[10]{0:T(128)}, u32[]{:S(2)}) copy-start(s32[10]{0:T(128)} %constant.92.clone) | copy-start | bytes 124
  124.7 65.2 %copy-start.6 = (s32[10]{0:T(128)S(1)}, s32[10]{0:T(128)}, u32[]{:S(2)}) copy-start(s32[10]{0:T(128)} %constant.93.clone) | copy-start | bytes 124
  124.7 253.9 %all-reduce.2.cloned.1.call-start = ((), (), s32[]{:S(2)}) async-start(), calls=%async_computation.2 | async-start | bytes 9437184 | tf_op jit(solution)/shard_map/psum | solution.py:52
  185.4 44.5 %collective-permute-start = (bf16[1024,1024]{0,1:T(8,128)(2,1)}, bf16[1024,1024]{0,1:T(8,128)(2,1)S(1)}, u32[]{:S(2)}, u32[]{:S(2)}) collective-permute-start(bf16[1024,1024]{0,1:T(8,128)(2,1)} %slice_bitcast_fusion), channel_id=1, source_target_pairs={{0,128},{1,129},{2,130},{3,131},{4,132},{5,133},{6,134},{7,135},{8... | collective-permute-start | bytes 6291464 | tf_op jit(solution)/shard_map/ppermute | solution.py:10
  229.9 3.8 copy-start.1
  233.7 4.7 %copy-start.3 = (bf16[5,1024,288]{1,2,0:T(8,128)(2,1)S(1)}, bf16[5,1024,288]{1,2,0:T(8,128)(2,1)}, u32[]{:S(2)}) copy-start(bf16[5,1024,288]{1,2,0:T(8,128)(2,1)} %param.12) | copy-start | bytes 8847364
  251.5 0.7 copy-start.8
  251.5 127.1 %copy-start.7 = (f32[4,288]{1,0:T(4,128)S(1)}, f32[4,288]{1,0:T(4,128)}, u32[]{:S(2)}) copy-start(f32[4,288]{1,0:T(4,128)} %param.13) | copy-start | bytes 13828
  378.6 4.2 %copy-start.2 = (bf16[1024,2,1024]{0,2,1:T(8,128)(2,1)S(1)}, bf16[1024,2,1024]{0,2,1:T(8,128)(2,1)}, u32[]{:S(2)}) copy-start(bf16[1024,2,1024]{0,2,1:T(8,128)(2,1)} %all-gather.5.cloned.1.call-done) | copy-start | bytes 12582916
  382.8 5.5 %copy-start.4 = (bf16[4,1024,288]{1,2,0:T(8,128)(2,1)}, bf16[4,1024,288]{1,2,0:T(8,128)(2,1)S(1)}, u32[]{:S(2)}) copy-start(bf16[4,1024,288]{1,2,0:T(8,128)(2,1)S(1)} %multiply_convert_fusion) | copy-start | bytes 7077892
  389.7 1.6 copy-start.9
Sparse Core Ops, SparseCore 0:
  9.8 107.5 all-gather.2
  124.8 57.5 all-gather.4
  251.6 126.9 all-reduce.1
where the time goes:
time: 398 us
  waiting for transfers between devices  321 us (81%)
  matrix products  26.5 us (7%)
  between operations  26.5 us (7%)
  local copies, waits for them, and re-layouts  15.5 us (4%)
  starting transfers between devices  4.52 us (1%)
    psum x1, waiting for transfers between devices, local(): summed = lax.psum(rebuilt, ('section', 'feat'))  126 us
    all_gather x1, waiting for transfers between devices, local(): lax.all_gather(encoder, 'width', axis=1, tiled=True)  109 us
    all_gather x1, waiting for transfers between devices, local(): token_feats = lax.all_gather(local_feats, 'width', axis=0, tiled=True)  57.6 us
    ppermute x1, waiting for transfers between devices, from_behind(): lax.ppermute(value, axis, [(source, source + steps) for source in range(i...  26.7 us
    dot_general x5, matrix products, local(): jnp.dot(picked, decoder[pair_slot], preferred_element_type=jnp.float32)  12.3 us
  transfers between devices with their start and end apart: 4, of which 4 were waited for; matrix products, arithmetic and copies ran while one was open for 0% of the time, Pallas kernels for 0%

commit v1 on v0

--- a/solution.py
+++ b/solution.py
@@ -49,7 +49,9 @@
         partial_value = jnp.dot(picked, decoder[pair_slot], preferred_element_type=jnp.float32)
         current = lax.dynamic_index_in_dim(rebuilt, target, 0, keepdims=False)
         rebuilt = lax.dynamic_update_index_in_dim(rebuilt, current + partial_value, target, 0)
-    summed = lax.psum(rebuilt, ("section", "feat"))
+    summed = rebuilt
+    for mesh_axis in ("feat", "section"):
+        summed = lax.psum(summed, mesh_axis)
     keep_rows = live_rows.astype(jnp.float32)[None, :, None]
     errors = ((summed + dec_bias[:, None, :] - targets.astype(jnp.float32)) * keep_rows).astype(
         jnp.bfloat16

time: 398 us -> 554 us (1.39)
  waiting for transfers between devices: 321 us -> 477 us
    psum x1 -> x2, waiting for transfers between devices: 126 us -> 282 us  [local(): summed = lax.psum(summed, mesh_axis)]
  transfers between devices with their start and end apart: 4 -> 5, of which waited for: 4 -> 5; matrix products, arithmetic and copies ran while one was open for 0% -> 0% of each run, Pallas kernels for 0% -> 0%
where the time goes in v1:
time: 554 us
  waiting for transfers between devices  477 us (86%)
  matrix products  26.5 us (5%)
  between operations  26.5 us (5%)
  local copies, waits for them, and re-layouts  15.5 us (3%)
    psum x2, waiting for transfers between devices, local(): summed = lax.psum(summed, mesh_axis)  282 us
    all_gather x1, waiting for transfers between devices, local(): lax.all_gather(encoder, 'width', axis=1, tiled=True)  109 us
    all_gather x1, waiting for transfers between devices, local(): token_feats = lax.all_gather(local_feats, 'width', axis=0, tiled=True)  57.6 us
    ppermute x1, waiting for transfers between devices, from_behind(): lax.ppermute(value, axis, [(source, source + steps) for source in range(i...  26.9 us
    dot_general x5, matrix products, local(): jnp.dot(picked, decoder[pair_slot], preferred_element_type=jnp.float32)  12.3 us
  transfers between devices with their start and end apart: 5, of which 5 were waited for; matrix products, arithmetic and copies ran while one was open for 0% of the time, Pallas kernels for 0%

profile of v1, /device:TPU:1, one launch (start us, length us, event | category | flops | bytes accessed | tf_op | source)
XLA Modules:
  0.0 553.9 jit_solution(1117009901755562962)
XLA Ops:
  7.2 0.0 copy-start
  7.2 0.0 all-gather.3.cloned.1.call-start
  7.2 0.7 all-gather.3.cloned.1.call-update
  7.9 0.0 all-gather.5.cloned.1.call-start
  8.0 109.4 %all-gather.3.cloned.1.call-done = bf16[2,2304,1024]{2,1,0:T(8,128)(2,1)} async-done(((bf16[2,288,1024]{2,1,0:T(8,128)(2,1)}), bf16[2,2304,1024]{2,1,0:T(8,128)(2,1)}) %all-gather.3.cloned.1.call-update) | async-done | bytes 9437200 | tf_op jit(solution)/shard_map/all_gather | solution.py:28
  117.3 0.0 copy-done
  117.3 7.3 %fusion.36 = bf16[128,2,1024]{0,2,1:T(8,128)(2,1)} fusion(bf16[2,2304,1024]{2,1,0:T(8,128)(2,1)} %all-gather.3.cloned.1.call-done, bf16[2,128,2304]{2,1,0:T(8,128)(2,1)S(1)} %copy-done, f32[2,1024]{1,0:T(2,128)} %param.11), kind=kOutput, calls=%fused_computation.59 | convolution fusion | flops 1208745984 | bytes 11149312 | tf_op jit(solution)/shard_map/ltd,ldf->tlf/dot_general | solution.py:25
  124.7 0.0 copy-start.5
  124.7 0.0 copy-start.6
  124.7 0.0 all-gather.5.cloned.1.call-update
  124.7 0.0 all-reduce.3.cloned.1.call-start
  124.7 57.6 %all-gather.5.cloned.1.call-done = bf16[1024,2,1024]{0,2,1:T(8,128)(2,1)} async-done(((bf16[128,2,1024]{0,2,1:T(8,128)(2,1)}), bf16[1024,2,1024]{0,2,1:T(8,128)(2,1)}) %all-gather.5.cloned.1.call-update) | async-done | bytes 4194320 | tf_op jit(solution)/shard_map/all_gather | solution.py:32
  182.4 3.1 slice_bitcast_fusion
  185.4 4.2 collective-permute-start
  189.7 0.0 copy-done.5
  189.7 0.0 copy-done.6
  189.7 0.7 fusion.72
  203.0 26.9 %collective-permute-done = bf16[1024,1024]{0,1:T(8,128)(2,1)S(1)} collective-permute-done((bf16[1024,1024]{0,1:T(8,128)(2,1)}, bf16[1024,1024]{0,1:T(8,128)(2,1)S(1)}, u32[]{:S(2)}, u32[]{:S(2)}) %collective-permute-start) | collective-permute-done | bytes 2097184 | tf_op jit(solution)/shard_map/ppermute | solution.py:10
  229.9 0.0 copy-start.1
  229.9 3.0 broadcast_in_dim.25
  232.9 0.8 copy-done.1
  233.7 0.0 copy-start.3
  233.7 3.4 fusion.18
  237.1 1.3 constant_dynamic-slice_fusion.3
  238.5 0.0 copy-done.3
  238.5 2.2 fusion.17
  240.7 1.3 constant_dynamic-slice_fusion.2
  242.1 2.2 fusion.15
  244.3 1.3 constant_dynamic-slice_fusion.1
  245.6 2.3 fusion.13
  247.9 1.3 constant_dynamic-slice_fusion
  249.3 2.2 fusion.11
  251.5 0.0 all-reduce.3.cloned.1.call-update
  251.5 0.2 all-reduce.5.cloned.1.call-start
  251.7 146.7 %all-reduce.3.cloned.1.call-done = f32[4,1024,288]{1,2,0:T(8,128)} async-done(((f32[4,1024,288]{1,2,0:T(8,128)}), f32[4,1024,288]{1,2,0:T(8,128)}) %all-reduce.3.cloned.1.call-update) | async-done | bytes 4718608 | tf_op jit(solution)/shard_map/psum | solution.py:54
  398.4 0.0 copy-start.8
  398.4 0.0 copy-start.7
  398.4 0.0 all-reduce.5.cloned.1.call-update
  398.5 0.7 copy-done.8
  399.1 135.5 %all-reduce.5.cloned.1.call-done = f32[4,1024,288]{1,2,0:T(8,128)} async-done(((f32[4,1024,288]{1,2,0:T(8,128)}), f32[4,1024,288]{1,2,0:T(8,128)}) %all-reduce.5.cloned.1.call-update) | async-done | bytes 4718608 | tf_op jit(solution)/shard_map/psum | solution.py:54
  534.6 0.0 copy-done.7
  534.6 0.0 copy-start.2
  534.6 3.9 multiply_convert_fusion
  538.6 0.3 copy-done.2
  538.9 0.0 copy-start.4
  538.9 1.4 fusion.35
  540.2 1.4 fusion.33
  541.6 1.4 fusion.31
  543.0 1.4 fusion.29
  544.4 0.0 copy-done.4
  544.4 1.4 fusion.27
  545.8 0.0 copy-start.9
  545.8 1.6 copy-done.9
  (1 shorter events, 0.0 us)
Async XLA Ops:
  7.2 110.2 %copy-start = (bf16[2,128,2304]{2,1,0:T(8,128)(2,1)S(1)}, bf16[2,128,2304]{2,1,0:T(8,128)(2,1)}, u32[]{:S(2)}) copy-start(bf16[2,128,2304]{2,1,0:T(8,128)(2,1)} %param.9) | copy-start | bytes 3538948
  7.2 110.2 %all-gather.3.cloned.1.call-start = ((), (), s32[]{:S(2)}) async-start(), calls=%async_computation | async-start | bytes 10616832 | tf_op jit(solution)/shard_map/all_gather | solution.py:28
  7.9 174.4 %all-gather.5.cloned.1.call-start = ((), (), s32[]{:S(2)}) async-start(), calls=%async_computation.1 | async-start | bytes 4718592 | tf_op jit(solution)/shard_map/all_gather | solution.py:32
  124.7 65.0 %copy-start.5 = (s32[10]{0:T(128)S(1)}, s32[10]{0:T(128)}, u32[]{:S(2)}) copy-start(s32[10]{0:T(128)} %constant.92.clone) | copy-start | bytes 124
  124.7 65.0 %copy-start.6 = (s32[10]{0:T(128)S(1)}, s32[10]{0:T(128)}, u32[]{:S(2)}) copy-start(s32[10]{0:T(128)} %constant.93.clone) | copy-start | bytes 124
  124.7 273.8 %all-reduce.3.cloned.1.call-start = ((), (), s32[]{:S(2)}) async-start(), calls=%async_computation.2 | async-start | bytes 9437184 | tf_op jit(solution)/shard_map/psum | solution.py:54
  185.4 44.5 %collective-permute-start = (bf16[1024,1024]{0,1:T(8,128)(2,1)}, bf16[1024,1024]{0,1:T(8,128)(2,1)S(1)}, u32[]{:S(2)}, u32[]{:S(2)}) collective-permute-start(bf16[1024,1024]{0,1:T(8,128)(2,1)} %slice_bitcast_fusion), channel_id=1, source_target_pairs={{0,128},{1,129},{2,130},{3,131},{4,132},{5,133},{6,134},{7,135},{8... | collective-permute-start | bytes 6291464 | tf_op jit(solution)/shard_map/ppermute | solution.py:10
  229.9 3.8 copy-start.1
  233.7 4.7 copy-start.3
  251.5 283.1 %all-reduce.5.cloned.1.call-start = ((), (), s32[]{:S(2)}) async-start(), calls=%async_computation.3 | async-start | bytes 9437184 | tf_op jit(solution)/shard_map/psum | solution.py:54
  398.4 0.7 copy-start.8
  398.4 136.2 %copy-start.7 = (f32[4,288]{1,0:T(4,128)S(1)}, f32[4,288]{1,0:T(4,128)}, u32[]{:S(2)}) copy-start(f32[4,288]{1,0:T(4,128)} %param.13) | copy-start | bytes 13828
  534.6 4.2 copy-start.2
  538.9 5.5 copy-start.4
  545.8 1.6 copy-start.9
Sparse Core Ops, SparseCore 0:
  9.8 107.5 all-gather.2
  124.8 57.5 all-gather.4
  251.6 146.7 all-reduce.2
  401.0 133.5 all-reduce.4
